TPU v7x, 32 devices: a whole 2x2x4 slice. The times are simulated.
32 devices in a mesh: wide: 8 (over z, core), narrow: 4 (over y, x).
Axes of the slice: x: 2, y: 2, z: 4, core: 2. Of those that a mesh axis runs over, the one named last changes fastest.
Arguments:
- operator: bfloat16 [8, 4, 2, 2048, 2048], P('wide', 'narrow'), may hold values from -0.125 to 0.125
- sources: bfloat16 [8, 4, 2048, 128], P('wide', 'narrow'), may hold values from -6 to 6
- face_lengths: int32 [8, 4, 4], P('wide', 'narrow'), may hold values from 192 to 640, as said below
Outputs:
- outgoing: bfloat16 [8, 4, 2048, 128], P('wide', 'narrow')
- incoming: bfloat16 [8, 4, 2048, 128], P('wide', 'narrow')
Inputs may be any that keep to these rules, and one draw needn't show every extreme that they name: `face_lengths`: the entries of adjacent subdomains for their common face are equal; lower-row and higher-row entries lie in 320 to 640, column entries in 192 to 384.
All inputs are finite; a program needn't handle non-finite values.
Results may differ from a plain program's by a relative error of at most 0.0055.
Values may be sent and summed in bfloat16 or wider, within the bound.
A program may use at most 64 MiB of HBM per device.

v0:
```python
import functools

import jax
import jax.numpy as jnp
from jax import lax
from jax.experimental import pallas as pl
from jax.experimental.pallas import tpu as pltpu
from jax.sharding import PartitionSpec as P

FACE_LONG = 640
FACE_SHORT = 384
ITERS = 3
TILE = 1024
MESH = pl.DeviceIdType.MESH


def kernel(n_wide, n_narrow, oper_hbm, src_hbm, len_ref, last_out, last_in,
           w, src, xs, acc, outs,
           w_sem, src_sem, send_sem, recv_sem):
    total = src.shape[0]
    short0 = 2 * FACE_LONG
    row = lax.axis_index("wide")
    col = lax.axis_index("narrow")
    far = lax.rem(row, 2)
    near = 1 - far
    first = jnp.where(2 * col < n_narrow, 1, 0)
    second = 1 - first

    def long_off(face):
        return pl.multiple_of(face * FACE_LONG, 128)

    def short_off(face):
        return pl.multiple_of(short0 + face * FACE_SHORT, 128)

    def geometry(is_long, face):
        if is_long:
            target = row + 2 * face - 1
            return (long_off(face), long_off(1 - face), FACE_LONG, {"wide": target},
                    (target >= 0) & (target < n_wide), face)
        target = col + 2 * face - 1
        return (short_off(face), short_off(1 - face), FACE_SHORT, {"narrow": target},
                (target >= 0) & (target < n_narrow), 2 + face)

    def sent_from(step):
        return src if step == 0 else last_out if step == ITERS else outs.at[step - 1]

    def landed_in(step):
        return last_in if step == ITERS else xs.at[step]

    def landing(step, there):
        return there if step == ITERS else pl.multiple_of(2 * there, 128)

    faces = [(False, first), (False, second), (True, far), (True, near)]

    def send(step, is_long, face, start):
        here, there, size, device, exists, slot = geometry(is_long, face)
        other = (2 + 1 - face) if is_long is False else 1 - face
        source, target = sent_from(step), landed_in(step)
        copy = pltpu.make_async_remote_copy(
            src_ref=source.at[pl.ds(here, size)],
            dst_ref=target.at[pl.ds(landing(step, there), size)],
            send_sem=send_sem.at[step, slot],
            recv_sem=recv_sem.at[step, other],
            device_id=device,
            device_id_type=MESH,
        )

        @pl.when(exists)
        def _():
            if start:
                copy.start()
            else:
                copy.wait_send()

    def receive(step, is_long, face):
        here, there, size, device, exists, slot = geometry(is_long, face)
        source, target = sent_from(step), landed_in(step)
        copy = pltpu.make_async_remote_copy(
            src_ref=source.at[pl.ds(here, size)],
            dst_ref=target.at[pl.ds(landing(step, here), size)],
            send_sem=send_sem.at[step, slot],
            recv_sem=recv_sem.at[step, slot],
            device_id=device,
            device_id_type=MESH,
        )

        @pl.when(exists)
        def _():
            copy.wait_recv()

    src_copy = pltpu.make_async_copy(src_hbm.at[0, 0], src, src_sem)
    src_copy.start()

    barrier = pltpu.get_barrier_semaphore()
    count = jnp.int32(0)
    for is_long, face in faces:
        _, _, _, device, exists, _ = geometry(is_long, face)
        count = count + exists.astype(jnp.int32)

        @pl.when(exists)
        def _():
            pl.semaphore_signal(barrier, inc=1, device_id=device, device_id_type=MESH)

    def loads(is_long, face):
        here, _, size, _, _, slot = geometry(is_long, face)
        return [pltpu.make_async_copy(
            oper_hbm.at[0, 0, part, :, pl.ds(here, size)],
            w.at[:, pl.ds(pl.multiple_of(2 * here + part * size, 128), size)],
            w_sem.at[part, slot]) for part in range(2)]

    def load(is_long, face):
        for copy in loads(is_long, face):
            copy.start()

    def loaded(is_long, face):
        for copy in loads(is_long, face):
            copy.wait()

    load(True, near)

    pl.semaphore_wait(barrier, count)
    src_copy.wait()
    for is_long, face in faces:
        send(0, is_long, face, True)

    load(True, far)
    load(False, 0)
    load(False, 1)

    for is_long, face in faces:
        here, _, size, _, exists, slot = geometry(is_long, face)

        @pl.when(jnp.logical_not(exists))
        def _():
            for step in range(ITERS + 1):
                rows = pl.ds(landing(step, here), size)
                landed_in(step)[rows, :] = jnp.zeros((size, xs.shape[2]), xs.dtype)

    def live(slot, size):
        return lax.broadcasted_iota(jnp.int32, (size, xs.shape[2]), 0) < len_ref[0, 0, slot]

    half = xs.shape[2] // 2

    def prepare(step, is_long, face):
        here, _, size, _, _, slot = geometry(is_long, face)
        rows = pl.ds(landing(step, here), size)
        value = xs[step, rows, :].astype(jnp.float32)
        if step == 0:
            value = jnp.where(live(slot, size), value, 0.0)
            xs[step, rows, :] = value.astype(xs.dtype)
        lanes = lax.broadcasted_iota(jnp.int32, value.shape, 1)
        turned = pltpu.roll(value, half, 1)
        rows = pl.ds(pl.multiple_of(2 * here + size, 128), size)
        xs[step, rows, :] = jnp.where(lanes < half, -turned, turned).astype(xs.dtype)

    def product(step, rows, cols):
        return jnp.dot(w[rows, cols], xs[step, cols, :], preferred_element_type=jnp.float32)

    for step in range(ITERS):
        for which, face in ((0, near), (1, far)):
            if step == 0:
                loaded(True, face)
            receive(step, True, face)
            prepare(step, True, face)
            cols = pl.ds(pl.multiple_of(2 * long_off(face), 128), 2 * FACE_LONG)

            @pl.loop(0, total // TILE)
            def _(tile):
                rows = pl.ds(pl.multiple_of(tile * TILE, TILE), TILE)
                base = src[rows, :].astype(jnp.float32) if which == 0 else acc[rows, :]
                acc[rows, :] = base + product(step, rows, cols)

        for face in (0, 1):
            if step == 0:
                loaded(False, face)
        for face in (0, 1):
            receive(step, False, face)
            prepare(step, False, face)
        cols = pl.ds(2 * short0, 4 * FACE_SHORT)
        for is_long, face in faces:
            here, _, size, _, _, slot = geometry(is_long, face)
            rows = pl.ds(here, size)
            value = acc[rows, :] + product(step, rows, cols)
            sent_from(step + 1)[rows, :] = jnp.where(live(slot, size), value, 0.0).astype(xs.dtype)
            send(step + 1, is_long, face, True)

    for step in range(ITERS + 1):
        for is_long, face in faces:
            send(step, is_long, face, False)
    for is_long, face in faces:
        receive(ITERS, is_long, face)


def write_out(out_ref, in_ref, out_hbm, in_hbm, sem):
    copies = [pltpu.make_async_copy(out_ref, out_hbm.at[0, 0], sem.at[0]),
              pltpu.make_async_copy(in_ref, in_hbm.at[0, 0], sem.at[1])]
    for copy in copies:
        copy.start()
    for copy in copies:
        copy.wait()


def body(n_wide, n_narrow, operator, sources, face_lengths):
    total, width = sources.shape[2:]
    dtype = sources.dtype
    held = pltpu.VMEM((total, width), dtype)
    outgoing, incoming = pl.pallas_call(
        functools.partial(kernel, n_wide, n_narrow),
        out_shape=(held, held),
        in_specs=[
            pl.BlockSpec(memory_space=pltpu.HBM),
            pl.BlockSpec(memory_space=pltpu.HBM),
            pl.BlockSpec(memory_space=pltpu.SMEM),
        ],
        out_specs=[pl.BlockSpec(memory_space=pltpu.VMEM)] * 2,
        scratch_shapes=[
            pltpu.VMEM((total, 2 * total), dtype),
            pltpu.VMEM((total, width), dtype),
            pltpu.VMEM((ITERS, 2 * total, width), dtype),
            pltpu.VMEM((total, width), jnp.float32),
            pltpu.VMEM((ITERS - 1, total, width), dtype),
            pltpu.SemaphoreType.DMA((2, 4)),
            pltpu.SemaphoreType.DMA,
            pltpu.SemaphoreType.DMA((ITERS + 1, 4)),
            pltpu.SemaphoreType.DMA((ITERS + 1, 4)),
        ],
        compiler_params=pltpu.CompilerParams(
            collective_id=0, has_side_effects=True, vmem_limit_bytes=54 * 1024 * 1024),
        name="schwarz",
    )(operator, sources, face_lengths)
    shape = jax.ShapeDtypeStruct(sources.shape, dtype)
    return pl.pallas_call(
        write_out,
        out_shape=(shape, shape),
        in_specs=[pl.BlockSpec(memory_space=pltpu.VMEM)] * 2,
        out_specs=[pl.BlockSpec(memory_space=pl.ANY)] * 2,
        scratch_shapes=[pltpu.SemaphoreType.DMA((2,))],
        compiler_params=pltpu.CompilerParams(vmem_limit_bytes=4 * 1024 * 1024),
        name="write_out",
    )(outgoing, incoming)


def solution(mesh):
    in_specs = (
        P("wide", "narrow", None, None, None),
        P("wide", "narrow", None, None),
        P("wide", "narrow", None),
    )
    out_specs = (P("wide", "narrow", None, None), P("wide", "narrow", None, None))
    step = functools.partial(body, mesh.shape["wide"], mesh.shape["narrow"])
    return jax.shard_map(step, mesh=mesh, in_specs=in_specs, out_specs=out_specs, check_vma=False)
```

profile of v0, /device:TPU:1, one launch (start us, length us, event | category | flops | bytes accessed | tf_op | source)
XLA Modules:
  0.0 33.5 jit_solution(9189421350814201587)
XLA Ops:
  0.6 31.9 %schwarz.1 = (bf16[2048,128]{1,0:T(8,128)(2,1)S(1)}, bf16[2048,128]{1,0:T(8,128)(2,1)S(1)}) custom-call(bf16[1,1,2,2048,2048]{4,3,2,1,0:T(8,128)(2,1)} %oper_hbm.1, bf16[1,1,2048,128]{3,2,1,0:T(8,128)(2,1)} %src_hbm.1, s32[1,1,4]{2,1,0:T(1,128)} %len_ref.1), custom_call_target="tpu_custom_call" | custom-call | tf_op jit(solution)/shard_map/schwarz/pallas_call | solution.py:207
  32.5 1.0 %write_out.1 = (bf16[1,1,2048,128]{3,2,1,0:T(8,128)(2,1)}, bf16[1,1,2048,128]{3,2,1,0:T(8,128)(2,1)}) custom-call(bf16[2048,128]{1,0:T(8,128)(2,1)S(1)} %get-tuple-element.4.out_ref, bf16[2048,128]{1,0:T(8,128)(2,1)S(1)} %get-tuple-element.5.in_ref), custom_call_target="tpu_custom_call" | custom-call | tf_op jit(solution)/shard_map/write_out/pallas_call | solution.py:232
where the time goes:
time: 33.7 us; the launch traced here: 33.5 us
  Pallas kernels  32.9 us (98%)
  between operations  0.64 us (2%)
    pallas_call x1, Pallas kernels, body(): pl.pallas_call(functools.partial(kernel, n_wide, n_narrow), out_shape=(he...  31.9 us
    pallas_call x1, Pallas kernels, body(): pl.pallas_call(write_out, out_shape=(shape, shape), in_specs=[pl.BlockSpe...  0.99 us

commit v1 on v0

v1 whole, which is shorter than its diff:
```python
import functools

import jax
import jax.numpy as jnp
from jax import lax
from jax.experimental import pallas as pl
from jax.experimental.pallas import tpu as pltpu
from jax.sharding import PartitionSpec as P

FACE_LONG = 640
FACE_SHORT = 384
ITERS = 3
CHUNK = 128
EARLY = 3
MESH = pl.DeviceIdType.MESH


def kernel(n_wide, n_narrow, oper_hbm, src_hbm, len_ref, last_out, last_in,
           stage, wt, src, src_t, landed, xs, acc, out_long, out_short,
           w_sem, src_sem, send_sem, recv_sem):
    total, width = src.shape
    half = width // 2
    short0 = 2 * FACE_LONG
    far_k, short_k = 2 * FACE_LONG, 4 * FACE_LONG
    far_n, near_n = 2 * FACE_SHORT, 2 * FACE_SHORT + FACE_LONG
    chunks = total // CHUNK
    row = lax.axis_index("wide")
    col = lax.axis_index("narrow")
    far = lax.rem(row, 2)
    near = 1 - far
    first = jnp.where(2 * col < n_narrow, 1, 0)
    second = 1 - first

    def long_off(face):
        return pl.multiple_of(face * FACE_LONG, 128)

    def short_off(face):
        return pl.multiple_of(short0 + face * FACE_SHORT, 128)

    faces = [(False, first, None), (False, second, None), (True, far, 1), (True, near, 0)]

    def geometry(is_long, face):
        if is_long:
            target = row + 2 * face - 1
            return (long_off(face), long_off(1 - face), FACE_LONG, {"wide": target},
                    (target >= 0) & (target < n_wide), face, 1 - face)
        target = col + 2 * face - 1
        return (short_off(face), short_off(1 - face), FACE_SHORT, {"narrow": target},
                (target >= 0) & (target < n_narrow), 2 + face, 3 - face)

    def k_off(is_long, face, role):
        if is_long:
            return role * far_k
        return pl.multiple_of(short_k + face * 2 * FACE_SHORT, 128)

    def ends(step, is_long, face, role, sending):
        here, there, size, device, exists, slot, other = geometry(is_long, face)
        if step in (0, ITERS):
            source = (src if step == 0 else last_out).at[pl.ds(here, size)]
            target = (landed if step == 0 else last_in).at[pl.ds(there if sending else here, size)]
        else:
            source = out_long.at[step - 1, role] if is_long else out_short.at[step - 1, face]
            at = k_off(is_long, 1 - face if sending else face, role)
            target = xs.at[step, :, pl.ds(at, size)]
        copy = pltpu.make_async_remote_copy(
            src_ref=source,
            dst_ref=target,
            send_sem=send_sem.at[step, slot],
            recv_sem=recv_sem.at[step, other if sending else slot],
            device_id=device,
            device_id_type=MESH,
        )
        return copy, exists

    def send(step, is_long, face, role, start):
        copy, exists = ends(step, is_long, face, role, True)

        @pl.when(exists)
        def _():
            if start:
                copy.start()
            else:
                copy.wait_send()

    def receive(step, is_long, face, role):
        copy, exists = ends(step, is_long, face, role, False)

        @pl.when(exists)
        def _():
            copy.wait_recv()

    src_copy = pltpu.make_async_copy(src_hbm.at[0, 0], src, src_sem)
    src_copy.start()

    barrier = pltpu.get_barrier_semaphore()
    count = jnp.int32(0)
    for is_long, face, _ in faces:
        _, _, _, device, exists, _, _ = geometry(is_long, face)
        count = count + exists.astype(jnp.int32)

        @pl.when(exists)
        def _():
            pl.semaphore_signal(barrier, inc=1, device_id=device, device_id_type=MESH)

    def load(n):
        shorts = far_n // CHUNK
        longs = FACE_LONG // CHUNK
        at = jnp.where(n < shorts, short0 + n * CHUNK,
                       jnp.where(n < shorts + longs, far * FACE_LONG + (n - shorts) * CHUNK,
                                 near * FACE_LONG + (n - shorts - longs) * CHUNK))
        return pltpu.make_async_copy(
            oper_hbm.at[0, 0, :, pl.ds(pl.multiple_of(at, CHUNK), CHUNK), :],
            stage.at[n], w_sem.at[n])

    @pl.loop(0, EARLY)
    def _(n):
        load(n).start()

    src_copy.wait()
    pl.semaphore_wait(barrier, count)
    for face in faces:
        send(0, *face, True)

    @pl.loop(EARLY, chunks)
    def _(n):
        load(n).start()

    def live(slot, shape):
        return lax.broadcasted_iota(jnp.int32, shape, 1) < len_ref[0, 0, slot]

    def masked(value, slot):
        return jnp.where(live(slot, value.shape), value, 0.0)

    for is_long, face, role in faces:
        here, _, size, _, exists, _, _ = geometry(is_long, face)

        @pl.when(jnp.logical_not(exists))
        def _():
            landed[pl.ds(here, size), :] = jnp.zeros((size, width), landed.dtype)
            last_in[pl.ds(here, size), :] = jnp.zeros((size, width), last_in.dtype)
            for step in range(1, ITERS):
                xs[step, :, pl.ds(k_off(is_long, face, role), size)] = jnp.zeros((width, size), xs.dtype)

    src_t[:, pl.ds(0, far_n)] = src[pl.ds(short0, far_n), :].T
    src_t[:, pl.ds(far_n, FACE_LONG)] = src[pl.ds(long_off(far), FACE_LONG), :].T
    src_t[:, pl.ds(near_n, FACE_LONG)] = src[pl.ds(long_off(near), FACE_LONG), :].T

    blocks = [(long_off(near), FACE_LONG, 0), (long_off(far), FACE_LONG, far_k),
              (short0, FACE_SHORT, short_k), (short0 + FACE_SHORT, FACE_SHORT, short_k + 2 * FACE_SHORT)]

    @pl.loop(0, chunks)
    def _(n):
        load(n).wait()
        cols = pl.ds(pl.multiple_of(n * CHUNK, CHUNK), CHUNK)
        for part in range(2):
            for at, size, k in blocks:
                wt[pl.ds(k + part * size, size), cols] = stage[n, part, :, pl.ds(at, size)].T

    def prepare(step, is_long, face, role):
        here, _, size, _, _, slot, _ = geometry(is_long, face)
        at = k_off(is_long, face, role)
        if step == 0:
            value = masked(landed[pl.ds(here, size), :].T.astype(jnp.float32), slot).astype(xs.dtype)
            xs[step, :, pl.ds(at, size)] = value
        else:
            value = xs[step, :, pl.ds(at, size)]
        turned = jnp.concatenate([-value[half:], value[:half]], axis=0)
        xs[step, :, pl.ds(pl.multiple_of(at + size, 128), size)] = turned

    def product(step, k, depth, n, cols):
        return jnp.dot(xs[step, :, pl.ds(k, depth)], wt[pl.ds(k, depth), pl.ds(n, cols)],
                       preferred_element_type=jnp.float32)

    def finish(step, is_long, face, role, value):
        here, _, size, _, _, slot, _ = geometry(is_long, face)
        value = masked(value, slot).astype(xs.dtype)
        if step == ITERS:
            last_out[pl.ds(here, size), :] = value.T
        elif is_long:
            out_long[step - 1, role] = value
        else:
            out_short[step - 1, face] = value

    for step in range(ITERS):
        for face, role in ((near, 0), (far, 1)):
            receive(step, True, face, role)
            prepare(step, True, face, role)
            for n in range(0, total, 512):
                base = src_t[:, pl.ds(n, 512)].astype(jnp.float32) if role == 0 else acc[:, pl.ds(n, 512)]
                acc[:, pl.ds(n, 512)] = base + product(step, role * far_k, far_k, n, 512)
        for face in (second, first):
            receive(step, False, face, None)
        for face in (0, 1):
            prepare(step, False, face, None)
        depth = 4 * FACE_SHORT
        value = acc[:, pl.ds(0, far_n)] + product(step, short_k, depth, 0, far_n)
        for face in (0, 1):
            finish(step + 1, False, face, None, value[:, face * FACE_SHORT:(face + 1) * FACE_SHORT])
        send(step + 1, *faces[0], True)
        send(step + 1, *faces[1], True)
        value = acc[:, pl.ds(far_n, 768)] + product(step, short_k, depth, far_n, 768)
        finish(step + 1, True, far, 1, value[:, :FACE_LONG])
        send(step + 1, *faces[2], True)
        rest = acc[:, pl.ds(far_n + 768, 512)] + product(step, short_k, depth, far_n + 768, 512)
        finish(step + 1, True, near, 0, jnp.concatenate([value[:, FACE_LONG:], rest], axis=1))
        send(step + 1, *faces[3], True)

    for step in range(ITERS + 1):
        for face in faces:
            send(step, *face, False)
    for face in faces[::-1]:
        receive(ITERS, *face)


def write_out(out_ref, in_ref, out_hbm, in_hbm, sem):
    copies = [pltpu.make_async_copy(out_ref, out_hbm.at[0, 0], sem.at[0]),
              pltpu.make_async_copy(in_ref, in_hbm.at[0, 0], sem.at[1])]
    for copy in copies:
        copy.start()
    for copy in copies:
        copy.wait()


def body(n_wide, n_narrow, operator, sources, face_lengths):
    total, width = sources.shape[2:]
    dtype = sources.dtype
    held = pltpu.VMEM((total, width), dtype)
    outgoing, incoming = pl.pallas_call(
        functools.partial(kernel, n_wide, n_narrow),
        out_shape=(held, held),
        in_specs=[
            pl.BlockSpec(memory_space=pltpu.HBM),
            pl.BlockSpec(memory_space=pltpu.HBM),
            pl.BlockSpec(memory_space=pltpu.SMEM),
        ],
        out_specs=[pl.BlockSpec(memory_space=pltpu.VMEM)] * 2,
        scratch_shapes=[
            pltpu.VMEM((total // CHUNK, 2, CHUNK, total), dtype),
            pltpu.VMEM((2 * total, total), dtype),
            pltpu.VMEM((total, width), dtype),
            pltpu.VMEM((width, total), dtype),
            pltpu.VMEM((total, width), dtype),
            pltpu.VMEM((ITERS, width, 2 * total), dtype),
            pltpu.VMEM((width, total), jnp.float32),
            pltpu.VMEM((ITERS - 1, 2, width, FACE_LONG), dtype),
            pltpu.VMEM((ITERS - 1, 2, width, FACE_SHORT), dtype),
            pltpu.SemaphoreType.DMA((total // CHUNK,)),
            pltpu.SemaphoreType.DMA,
            pltpu.SemaphoreType.DMA((ITERS + 1, 4)),
            pltpu.SemaphoreType.DMA((ITERS + 1, 4)),
        ],
        compiler_params=pltpu.CompilerParams(
            collective_id=0, has_side_effects=True, vmem_limit_bytes=54 * 1024 * 1024),
        name="schwarz",
    )(operator, sources, face_lengths)
    shape = jax.ShapeDtypeStruct(sources.shape, dtype)
    return pl.pallas_call(
        write_out,
        out_shape=(shape, shape),
        in_specs=[pl.BlockSpec(memory_space=pltpu.VMEM)] * 2,
        out_specs=[pl.BlockSpec(memory_space=pl.ANY)] * 2,
        scratch_shapes=[pltpu.SemaphoreType.DMA((2,))],
        compiler_params=pltpu.CompilerParams(vmem_limit_bytes=4 * 1024 * 1024),
        name="write_out",
    )(outgoing, incoming)


def solution(mesh):
    in_specs = (
        P("wide", "narrow", None, None, None),
        P("wide", "narrow", None, None),
        P("wide", "narrow", None),
    )
    out_specs = (P("wide", "narrow", None, None), P("wide", "narrow", None, None))
    step = functools.partial(body, mesh.shape["wide"], mesh.shape["narrow"])
    return jax.shard_map(step, mesh=mesh, in_specs=in_specs, out_specs=out_specs, check_vma=False)
```

time: 33.7 us -> 32.6 us (0.967)
  Pallas kernels: 32.9 us -> 31.8 us
    pallas_call x1, Pallas kernels: 31.9 us -> 30.8 us  [body(): pl.pallas_call(functools.partial(kernel, n_wide, n_narrow), out_shape=(he...]
where the time goes in v1:
time: 32.6 us; the launch traced here: 32.4 us
  Pallas kernels  31.8 us (98%)
  between operations  0.64 us (2%)
    pallas_call x1, Pallas kernels, body(): pl.pallas_call(functools.partial(kernel, n_wide, n_narrow), out_shape=(he...  30.8 us
    pallas_call x1, Pallas kernels, body(): pl.pallas_call(write_out, out_shape=(shape, shape), in_specs=[pl.BlockSpe...  0.99 us

profile of v1, /device:TPU:1, one launch (start us, length us, event | category | flops | bytes accessed | tf_op | source)
XLA Modules:
  0.0 32.4 jit_solution(6266927998886267769)
XLA Ops:
  0.6 30.8 %schwarz.1 = (bf16[2048,128]{1,0:T(8,128)(2,1)S(1)}, bf16[2048,128]{1,0:T(8,128)(2,1)S(1)}) custom-call(bf16[1,1,2,2048,2048]{4,3,2,1,0:T(8,128)(2,1)} %oper_hbm.1, bf16[1,1,2048,128]{3,2,1,0:T(8,128)(2,1)} %src_hbm.1, s32[1,1,4]{2,1,0:T(1,128)} %len_ref.1), custom_call_target="tpu_custom_call" | custom-call | tf_op jit(solution)/shard_map/schwarz/pallas_call | solution.py:228
  31.4 1.0 %write_out.1 = (bf16[1,1,2048,128]{3,2,1,0:T(8,128)(2,1)}, bf16[1,1,2048,128]{3,2,1,0:T(8,128)(2,1)}) custom-call(bf16[2048,128]{1,0:T(8,128)(2,1)S(1)} %get-tuple-element.4.out_ref, bf16[2048,128]{1,0:T(8,128)(2,1)S(1)} %get-tuple-element.5.in_ref), custom_call_target="tpu_custom_call" | custom-call | tf_op jit(solution)/shard_map/write_out/pallas_call | solution.py:257

commit v2 on v1

v2 whole, which is shorter than its diff:
```python
import functools

import jax
import jax.numpy as jnp
from jax import lax
from jax.experimental import pallas as pl
from jax.experimental.pallas import tpu as pltpu
from jax.sharding import PartitionSpec as P

FACE_LONG = 640
FACE_SHORT = 384
ITERS = 3
CHUNK = 128
EARLY = 8
WIDE = 256
MESH = pl.DeviceIdType.MESH


def kernel(n_wide, n_narrow, oper_hbm, src_hbm, len_hbm, last_out, last_in,
           stage, wt, src, src_t, landed, xs, acc, out_long, out_short, lens,
           w_sem, src_sem, len_sem, send_sem, recv_sem):
    total, width = src.shape
    half = width // 2
    short0 = 2 * FACE_LONG
    far_n, near_n = 2 * FACE_SHORT, 2 * FACE_SHORT + FACE_LONG
    long_k, short_k = 2 * FACE_LONG, 2 * FACE_SHORT
    near_k, second_k, far_k, first_k = 0, long_k, long_k + short_k, 2 * long_k + short_k
    chunks = total // CHUNK
    row = lax.axis_index("wide")
    col = lax.axis_index("narrow")
    far = lax.rem(row, 2)
    near = 1 - far

    def inward(at):
        return jnp.where(2 * at < n_narrow, 1, 0)

    first = inward(col)
    second = 1 - first

    def long_off(face):
        return pl.multiple_of(face * FACE_LONG, 128)

    def short_off(face):
        return pl.multiple_of(short0 + face * FACE_SHORT, 128)

    faces = [(False, first, first_k), (False, second, second_k), (True, far, far_k), (True, near, near_k)]

    def geometry(is_long, face):
        if is_long:
            target = row + 2 * face - 1
            return (long_off(face), long_off(1 - face), FACE_LONG, {"wide": target},
                    (target >= 0) & (target < n_wide), face, 1 - face)
        target = col + 2 * face - 1
        return (short_off(face), short_off(1 - face), FACE_SHORT, {"narrow": target},
                (target >= 0) & (target < n_narrow), 2 + face, 3 - face)

    def ends(step, is_long, face, k, sending):
        here, there, size, device, exists, slot, other = geometry(is_long, face)
        if step in (0, ITERS):
            source = (src if step == 0 else last_out).at[pl.ds(here, size)]
            target = (landed if step == 0 else last_in).at[pl.ds(there if sending else here, size)]
        else:
            source = out_long.at[step - 1, int(k == far_k)] if is_long else out_short.at[step - 1, face]
            if sending and not is_long:
                k = pl.multiple_of(jnp.where(1 - face == inward(col + 2 * face - 1), first_k, second_k), 128)
            target = xs.at[step, :, pl.ds(k, size)]
        copy = pltpu.make_async_remote_copy(
            src_ref=source,
            dst_ref=target,
            send_sem=send_sem.at[step, slot],
            recv_sem=recv_sem.at[step, other if sending else slot],
            device_id=device,
            device_id_type=MESH,
        )
        return copy, exists

    def send(step, is_long, face, k, start):
        copy, exists = ends(step, is_long, face, k, True)

        @pl.when(exists)
        def _():
            if start:
                copy.start()
            else:
                copy.wait_send()

    def receive(step, is_long, face, k):
        copy, exists = ends(step, is_long, face, k, False)

        @pl.when(exists)
        def _():
            copy.wait_recv()

    src_copy = pltpu.make_async_copy(src_hbm.at[0, 0], src, src_sem)
    src_copy.start()
    len_copy = pltpu.make_async_copy(len_hbm.at[0, 0], lens, len_sem)
    len_copy.start()

    barrier = pltpu.get_barrier_semaphore()
    count = jnp.int32(0)
    for is_long, face, _ in faces:
        _, _, _, device, exists, _, _ = geometry(is_long, face)
        count = count + exists.astype(jnp.int32)

        @pl.when(exists)
        def _():
            pl.semaphore_signal(barrier, inc=1, device_id=device, device_id_type=MESH)

    def load(n):
        shorts = far_n // CHUNK
        longs = FACE_LONG // CHUNK
        at = jnp.where(n < shorts, short0 + n * CHUNK,
                       jnp.where(n < shorts + longs, far * FACE_LONG + (n - shorts) * CHUNK,
                                 near * FACE_LONG + (n - shorts - longs) * CHUNK))
        return pltpu.make_async_copy(
            oper_hbm.at[0, 0, :, pl.ds(pl.multiple_of(at, CHUNK), CHUNK), :],
            stage.at[:, pl.ds(pl.multiple_of(n * CHUNK, CHUNK), CHUNK), :], w_sem.at[n])

    @pl.loop(0, EARLY)
    def _(n):
        load(n).start()

    src_copy.wait()
    pl.semaphore_wait(barrier, count)
    for face in faces:
        send(0, *face, True)

    @pl.loop(EARLY, chunks)
    def _(n):
        load(n).start()

    len_copy.wait()

    def masked(value, slot):
        slots = lax.broadcasted_iota(jnp.int32, value.shape, 1)
        return jnp.where(slots < lens[slot], value, 0.0)

    for is_long, face, k in faces:
        here, _, size, _, exists, _, _ = geometry(is_long, face)

        @pl.when(jnp.logical_not(exists))
        def _():
            landed[pl.ds(here, size), :] = jnp.zeros((size, width), landed.dtype)
            last_in[pl.ds(here, size), :] = jnp.zeros((size, width), last_in.dtype)
            for step in range(1, ITERS):
                xs[step, :, pl.ds(k, size)] = jnp.zeros((width, size), xs.dtype)

    src_t[:, pl.ds(0, far_n)] = src[pl.ds(short0, far_n), :].T
    src_t[:, pl.ds(far_n, FACE_LONG)] = src[pl.ds(long_off(far), FACE_LONG), :].T
    src_t[:, pl.ds(near_n, FACE_LONG)] = src[pl.ds(long_off(near), FACE_LONG), :].T

    blocks = [(long_off(near), FACE_LONG, near_k), (long_off(far), FACE_LONG, far_k),
              (short_off(second), FACE_SHORT, second_k), (short_off(first), FACE_SHORT, first_k)]

    def turn(n, which):
        for part in range(2):
            for at, size, k in which:
                wt[pl.ds(k + part * size, size), pl.ds(n * CHUNK, CHUNK)] = (
                    stage[part, pl.ds(n * CHUNK, CHUNK), pl.ds(at, size)].T)

    def arrive(step, is_long, face, k):
        receive(step, is_long, face, k)
        here, _, size, _, _, slot, _ = geometry(is_long, face)
        if step == 0:
            value = masked(landed[pl.ds(here, size), :].T.astype(jnp.float32), slot).astype(xs.dtype)
            xs[step, :, pl.ds(k, size)] = value
        else:
            value = xs[step, :, pl.ds(k, size)]
        xs[step, :, pl.ds(k + size, size)] = jnp.concatenate([-value[half:], value[:half]], axis=0)

    def product(step, k, depth, n, cols):
        return jnp.dot(xs[step, :, pl.ds(k, depth)], wt[pl.ds(k, depth), pl.ds(n, cols)],
                       preferred_element_type=jnp.float32)

    def add(step, k, depth, n, cols):
        base = src_t[:, pl.ds(n, cols)].astype(jnp.float32) if k == near_k else acc[:, pl.ds(n, cols)]
        acc[:, pl.ds(n, cols)] = base + product(step, k, depth, n, cols)

    def add_unturned(n):
        value = src_t[:, pl.ds(n, WIDE)].astype(jnp.float32)
        for part in range(2):
            value = value + lax.dot_general(
                xs[0, :, pl.ds(near_k + part * FACE_LONG, FACE_LONG)],
                stage[part, pl.ds(n, WIDE), pl.ds(long_off(near), FACE_LONG)],
                (((1,), (1,)), ((), ())), preferred_element_type=jnp.float32)
        acc[:, pl.ds(n, WIDE)] = value

    def finish(step, is_long, face, k, n):
        here, _, size, _, _, slot, _ = geometry(is_long, face)
        value = masked(acc[:, pl.ds(n, size)], slot).astype(xs.dtype)
        if step == ITERS:
            last_out[pl.ds(here, size), :] = value.T
        elif is_long:
            out_long[step - 1, int(k == far_k)] = value
        else:
            out_short[step - 1, face] = value

    def finish_shorts(step):
        for face in (0, 1):
            finish(step, False, face, None, face * FACE_SHORT)
        for face in faces[:2]:
            send(step, *face, True)

    def finish_far(step):
        finish(step, *faces[2], far_n)
        send(step, *faces[2], True)

    wide = 2 * FACE_SHORT

    for step in range(ITERS):
        if step == 0:
            per = WIDE // CHUNK
            groups = chunks // per
            for group in range(groups):
                if group == groups // 2:
                    arrive(0, *faces[3])
                for n in range(group * per, group * per + per):
                    load(n).wait()
                    turn(n, blocks[1:])
                if group >= groups // 2:
                    for g in range(2 * (group - groups // 2), 2 * (group - groups // 2) + 2):
                        add_unturned(g * WIDE)
        else:
            arrive(step, *faces[3])
            for n in range(0, total, WIDE):
                add(step, near_k, long_k, n, WIDE)
            for face in faces:
                send(step - 1, *face, False)
        arrive(step, *faces[1])
        add(step, second_k, short_k, 0, wide)
        arrive(step, *faces[2])
        add(step, far_k, long_k, 0, wide)
        arrive(step, *faces[0])
        add(step, first_k, short_k, 0, wide)
        finish_shorts(step + 1)
        add(step, second_k, long_k + 2 * short_k, wide, wide)
        finish_far(step + 1)
        add(step, second_k, long_k + 2 * short_k, 2 * wide, total - 2 * wide)
        finish(step + 1, *faces[3], near_n)
        send(step + 1, *faces[3], True)
        if step == 0:
            for n in range(chunks):
                turn(n, blocks[:1])

    for step in (ITERS - 1, ITERS):
        for face in faces:
            send(step, *face, False)
    for face in faces[::-1]:
        receive(ITERS, *face)


def write_out(out_ref, in_ref, out_hbm, in_hbm, sem):
    copies = [pltpu.make_async_copy(out_ref, out_hbm.at[0, 0], sem.at[0]),
              pltpu.make_async_copy(in_ref, in_hbm.at[0, 0], sem.at[1])]
    for copy in copies:
        copy.start()
    for copy in copies:
        copy.wait()


def body(n_wide, n_narrow, operator, sources, face_lengths):
    total, width = sources.shape[2:]
    dtype = sources.dtype
    held = pltpu.VMEM((total, width), dtype)
    outgoing, incoming = pl.pallas_call(
        functools.partial(kernel, n_wide, n_narrow),
        out_shape=(held, held),
        in_specs=[
            pl.BlockSpec(memory_space=pltpu.HBM),
            pl.BlockSpec(memory_space=pltpu.HBM),
            pl.BlockSpec(memory_space=pltpu.HBM),
        ],
        out_specs=[pl.BlockSpec(memory_space=pltpu.VMEM)] * 2,
        scratch_shapes=[
            pltpu.VMEM((2, total, total), dtype),
            pltpu.VMEM((2 * total, total), dtype),
            pltpu.VMEM((total, width), dtype),
            pltpu.VMEM((width, total), dtype),
            pltpu.VMEM((total, width), dtype),
            pltpu.VMEM((ITERS, width, 2 * total), dtype),
            pltpu.VMEM((width, total), jnp.float32),
            pltpu.VMEM((ITERS - 1, 2, width, FACE_LONG), dtype),
            pltpu.VMEM((ITERS - 1, 2, width, FACE_SHORT), dtype),
            pltpu.SMEM((4,), jnp.int32),
            pltpu.SemaphoreType.DMA((total // CHUNK,)),
            pltpu.SemaphoreType.DMA,
            pltpu.SemaphoreType.DMA,
            pltpu.SemaphoreType.DMA((ITERS + 1, 4)),
            pltpu.SemaphoreType.DMA((ITERS + 1, 4)),
        ],
        compiler_params=pltpu.CompilerParams(
            collective_id=0, has_side_effects=True, vmem_limit_bytes=54 * 1024 * 1024),
        name="schwarz",
    )(operator, sources, face_lengths)
    shape = jax.ShapeDtypeStruct(sources.shape, dtype)
    return pl.pallas_call(
        write_out,
        out_shape=(shape, shape),
        in_specs=[pl.BlockSpec(memory_space=pltpu.VMEM)] * 2,
        out_specs=[pl.BlockSpec(memory_space=pl.ANY)] * 2,
        scratch_shapes=[pltpu.SemaphoreType.DMA((2,))],
        compiler_params=pltpu.CompilerParams(vmem_limit_bytes=4 * 1024 * 1024),
        name="write_out",
    )(outgoing, incoming)


def solution(mesh):
    in_specs = (
        P("wide", "narrow", None, None, None),
        P("wide", "narrow", None, None),
        P("wide", "narrow", None),
    )
    out_specs = (P("wide", "narrow", None, None), P("wide", "narrow", None, None))
    step = functools.partial(body, mesh.shape["wide"], mesh.shape["narrow"])
    return jax.shard_map(step, mesh=mesh, in_specs=in_specs, out_specs=out_specs, check_vma=False)
```

time: 32.6 us -> 30.5 us (0.936)
  Pallas kernels: 31.8 us -> 29.4 us
    pallas_call x1, Pallas kernels: 30.8 us -> 28.4 us  [body(): pl.pallas_call(functools.partial(kernel, n_wide, n_narrow), out_shape=(he...]
where the time goes in v2:
time: 30.5 us; the launch traced here: 30 us
  Pallas kernels  29.4 us (96%)
  between operations  0.64 us (2%)
    pallas_call x1, Pallas kernels, body(): pl.pallas_call(functools.partial(kernel, n_wide, n_narrow), out_shape=(he...  28.4 us
    pallas_call x1, Pallas kernels, body(): pl.pallas_call(write_out, out_shape=(shape, shape), in_specs=[pl.BlockSpe...  0.99 us

profile of v2, /device:TPU:1, one launch (start us, length us, event | category | flops | bytes accessed | tf_op | source)
XLA Modules:
  0.0 30.0 jit_solution(3995809957129872810)
XLA Ops:
  0.6 28.4 %schwarz.1 = (bf16[2048,128]{1,0:T(8,128)(2,1)S(1)}, bf16[2048,128]{1,0:T(8,128)(2,1)S(1)}) custom-call(bf16[1,1,2,2048,2048]{4,3,2,1,0:T(8,128)(2,1)} %oper_hbm.1, bf16[1,1,2048,128]{3,2,1,0:T(8,128)(2,1)} %src_hbm.1, s32[1,1,4]{2,1,0:T(1,128)} %len_hbm.1), custom_call_target="tpu_custom_call" | custom-call | tf_op jit(solution)/shard_map/schwarz/pallas_call | solution.py:265
  29.0 1.0 %write_out.1 = (bf16[1,1,2048,128]{3,2,1,0:T(8,128)(2,1)}, bf16[1,1,2048,128]{3,2,1,0:T(8,128)(2,1)}) custom-call(bf16[2048,128]{1,0:T(8,128)(2,1)S(1)} %get-tuple-element.4.out_ref, bf16[2048,128]{1,0:T(8,128)(2,1)S(1)} %get-tuple-element.5.in_ref), custom_call_target="tpu_custom_call" | custom-call | tf_op jit(solution)/shard_map/write_out/pallas_call | solution.py:296

commit v3 on v2

--- a/solution.py
+++ b/solution.py
@@ -74,10 +74,10 @@
         )
         return copy, exists
 
-    def send(step, is_long, face, k, start):
+    def send(step, is_long, face, k, start, also=True):
         copy, exists = ends(step, is_long, face, k, True)
 
-        @pl.when(exists)
+        @pl.when(exists & also)
         def _():
             if start:
                 copy.start()
@@ -109,7 +109,9 @@
     def load(n):
         shorts = far_n // CHUNK
         longs = FACE_LONG // CHUNK
-        at = jnp.where(n < shorts, short0 + n * CHUNK,
+        half_way = shorts // 2
+        at = jnp.where(n < shorts, short0 + jnp.where(n < half_way, first * FACE_SHORT + n * CHUNK,
+                                                      second * FACE_SHORT + (n - half_way) * CHUNK),
                        jnp.where(n < shorts + longs, far * FACE_LONG + (n - shorts) * CHUNK,
                                  near * FACE_LONG + (n - shorts - longs) * CHUNK))
         return pltpu.make_async_copy(
@@ -122,7 +124,9 @@
 
     src_copy.wait()
     pl.semaphore_wait(barrier, count)
-    for face in faces:
+    for face in faces[:2]:
+        send(0, *face, True, far == 0)
+    for face in faces[2:]:
         send(0, *face, True)
 
     @pl.loop(EARLY, chunks)
@@ -145,9 +149,13 @@
             for step in range(1, ITERS):
                 xs[step, :, pl.ds(k, size)] = jnp.zeros((width, size), xs.dtype)
 
-    src_t[:, pl.ds(0, far_n)] = src[pl.ds(short0, far_n), :].T
+    src_t[:, pl.ds(0, FACE_SHORT)] = src[pl.ds(short_off(first), FACE_SHORT), :].T
+    src_t[:, pl.ds(FACE_SHORT, FACE_SHORT)] = src[pl.ds(short_off(second), FACE_SHORT), :].T
     src_t[:, pl.ds(far_n, FACE_LONG)] = src[pl.ds(long_off(far), FACE_LONG), :].T
     src_t[:, pl.ds(near_n, FACE_LONG)] = src[pl.ds(long_off(near), FACE_LONG), :].T
+
+    for face in faces[:2]:
+        send(0, *face, True, far == 1)
 
     blocks = [(long_off(near), FACE_LONG, near_k), (long_off(far), FACE_LONG, far_k),
               (short_off(second), FACE_SHORT, second_k), (short_off(first), FACE_SHORT, first_k)]
@@ -185,25 +193,19 @@
                 (((1,), (1,)), ((), ())), preferred_element_type=jnp.float32)
         acc[:, pl.ds(n, WIDE)] = value
 
-    def finish(step, is_long, face, k, n):
+    def finish(step, is_long, face, k, value):
         here, _, size, _, _, slot, _ = geometry(is_long, face)
-        value = masked(acc[:, pl.ds(n, size)], slot).astype(xs.dtype)
+        value = masked(value, slot).astype(xs.dtype)
         if step == ITERS:
             last_out[pl.ds(here, size), :] = value.T
         elif is_long:
             out_long[step - 1, int(k == far_k)] = value
         else:
             out_short[step - 1, face] = value
-
-    def finish_shorts(step):
-        for face in (0, 1):
-            finish(step, False, face, None, face * FACE_SHORT)
-        for face in faces[:2]:
-            send(step, *face, True)
-
-    def finish_far(step):
-        finish(step, *faces[2], far_n)
-        send(step, *faces[2], True)
+        send(step, is_long, face, k, True)
+
+    def closed(step, k, depth, n, cols):
+        return acc[:, pl.ds(n, cols)] + product(step, k, depth, n, cols)
 
     wide = 2 * FACE_SHORT
 
@@ -231,13 +233,13 @@
         arrive(step, *faces[2])
         add(step, far_k, long_k, 0, wide)
         arrive(step, *faces[0])
-        add(step, first_k, short_k, 0, wide)
-        finish_shorts(step + 1)
-        add(step, second_k, long_k + 2 * short_k, wide, wide)
-        finish_far(step + 1)
-        add(step, second_k, long_k + 2 * short_k, 2 * wide, total - 2 * wide)
-        finish(step + 1, *faces[3], near_n)
-        send(step + 1, *faces[3], True)
+        value = closed(step, first_k, short_k, 0, wide)
+        finish(step + 1, *faces[0], value[:, :FACE_SHORT])
+        finish(step + 1, *faces[1], value[:, FACE_SHORT:])
+        value = closed(step, second_k, long_k + 2 * short_k, wide, wide)
+        finish(step + 1, *faces[2], value[:, :FACE_LONG])
+        rest = closed(step, second_k, long_k + 2 * short_k, 2 * wide, total - 2 * wide)
+        finish(step + 1, *faces[3], jnp.concatenate([value[:, FACE_LONG:], rest], axis=1))
         if step == 0:
             for n in range(chunks):
                 turn(n, blocks[:1])

time: 30.5 us -> 30.4 us (level)
  no operation moved by 1% of the time
where the time goes in v3:
time: 30.4 us; the launch traced here: 30 us
  Pallas kernels  29.4 us (97%)
  between operations  0.64 us (2%)
    pallas_call x1, Pallas kernels, body(): pl.pallas_call(functools.partial(kernel, n_wide, n_narrow), out_shape=(he...  28.4 us
    pallas_call x1, Pallas kernels, body(): pl.pallas_call(write_out, out_shape=(shape, shape), in_specs=[pl.BlockSpe...  0.99 us

profile of v3, /device:TPU:1, one launch (start us, length us, event | category | flops | bytes accessed | tf_op | source)
XLA Modules:
  0.0 30.0 jit_solution(12734532843106509238)
XLA Ops:
  0.6 28.4 %schwarz.1 = (bf16[2048,128]{1,0:T(8,128)(2,1)S(1)}, bf16[2048,128]{1,0:T(8,128)(2,1)S(1)}) custom-call(bf16[1,1,2,2048,2048]{4,3,2,1,0:T(8,128)(2,1)} %oper_hbm.1, bf16[1,1,2048,128]{3,2,1,0:T(8,128)(2,1)} %src_hbm.1, s32[1,1,4]{2,1,0:T(1,128)} %len_hbm.1), custom_call_target="tpu_custom_call" | custom-call | tf_op jit(solution)/shard_map/schwarz/pallas_call | solution.py:267
  29.0 1.0 %write_out.1 = (bf16[1,1,2048,128]{3,2,1,0:T(8,128)(2,1)}, bf16[1,1,2048,128]{3,2,1,0:T(8,128)(2,1)}) custom-call(bf16[2048,128]{1,0:T(8,128)(2,1)S(1)} %get-tuple-element.4.out_ref, bf16[2048,128]{1,0:T(8,128)(2,1)S(1)} %get-tuple-element.5.in_ref), custom_call_target="tpu_custom_call" | custom-call | tf_op jit(solution)/shard_map/write_out/pallas_call | solution.py:298
